TPU v7x, 32 devices: a whole 2x2x4 slice. The times are simulated.
32 devices in a mesh: groups: 2 (over x), ctx: 16 (over z, y, core).
Axes of the slice: x: 2, y: 2, z: 4, core: 2. Of those that a mesh axis runs over, the one named last changes fastest.
Arguments:
- query_states: bfloat16 [16384, 32, 128], P(('groups', 'ctx')), parts along dimension 0, may hold values from -20 to 20
- key_states: bfloat16 [16384, 8, 128], P(('groups', 'ctx')), parts along dimension 0, may hold values from -4 to 4
- value_states: bfloat16 [16384, 8, 128], P(('groups', 'ctx')), parts along dimension 0, may hold values from -6 to 6
- vert_blocks: int32 [16, 4], P('groups'), parts along dimension 0, may hold values from 0 to 63, as said below
- vert_count: int32 [16], P('groups'), parts along dimension 0, may hold values from 1 to 4, as said below
- slash_offsets: int32 [16, 4], P('groups'), parts along dimension 0, may hold values from 0 to 8, as said below
- slash_count: int32 [16], P('groups'), parts along dimension 0, may hold values from 1 to 4, as said below
Outputs:
- attended: bfloat16 [16384, 32, 128], P(('groups', 'ctx')), parts along dimension 0
There are 2 independent parts, one for each index of `groups`. A program takes and returns all parts, laid end to end along the dimension named above; each array names one. Nothing has to cross between parts.
Inputs may be any that keep to these rules, and one draw needn't show every extreme that they name: `vert_blocks`: the 4 entries of each head are distinct; in some head the first entry lies in one of the first 4 blocks. `vert_count`: some head uses all 4 entries. `slash_offsets`: the 4 entries of each head are distinct and the first is 0. `slash_count`: some head uses all 4 entries.
All inputs are finite; a program needn't handle non-finite values.
Results may differ from a plain program's by a relative error of at most 0.0048.
Values may be sent and summed in bfloat16 or wider, within the bound.
A program may use at most 128 MiB of HBM per device.

v0:
```python
import functools
import math

import jax
import jax.numpy as jnp
from jax import lax
from jax.experimental import pallas as pl
from jax.experimental.pallas import tpu as pltpu
from jax.sharding import PartitionSpec as P

BLOCK = 128
REACH = 2


def attend_kernel(
    dims, vb_ref, vc_ref, so_ref, sc_ref, dev_ref, q_ref, kv_ref, out_ref, list_ref
):
    per_dev, n_vert, n_slash, group_size, head_dim = dims
    n_window = (REACH + 1) * per_dev
    head = pl.program_id(0)
    device = dev_ref[0]
    scale = math.log2(math.e) / math.sqrt(head_dim)
    rows = group_size * BLOCK
    in_tile = lax.broadcasted_iota(jnp.int32, (rows, BLOCK), 0) % BLOCK
    causal = lax.broadcasted_iota(jnp.int32, (rows, BLOCK), 1) <= in_tile

    def one_block(block, carry):
        qblock = device * per_dev + block
        count = jnp.int32(0)
        for v in range(n_vert):
            list_ref[count] = n_window + v
            ok = (v < vc_ref[head]) & (vb_ref[head, v] < qblock)
            count = count + ok.astype(jnp.int32)
        for s in range(1, n_slash):
            offset = so_ref[head, s]
            ok = (s < sc_ref[head]) & (offset <= qblock)
            for v in range(n_vert):
                ok = ok & ((v >= vc_ref[head]) | (vb_ref[head, v] != qblock - offset))
            list_ref[count] = REACH * per_dev + block - offset
            count = count + ok.astype(jnp.int32)

        start = pl.multiple_of(block * BLOCK, BLOCK)
        for n in range(n_vert + n_slash):

            @pl.when(count == n)
            def _(n=n):
                queries = jnp.concatenate(
                    [
                        q_ref[pl.ds(start, BLOCK), h * head_dim : (h + 1) * head_dim]
                        for h in range(group_size)
                    ],
                    axis=0,
                )
                spots = [REACH * per_dev + block] + [list_ref[i] for i in range(n)]
                scores = []
                for i, spot in enumerate(spots):
                    tile = lax.dot_general(
                        queries,
                        kv_ref[0, spot, 0],
                        (((1,), (1,)), ((), ())),
                        preferred_element_type=jnp.float32,
                    )
                    scores.append(jnp.where(causal, tile, -1e30) if i == 0 else tile)
                top = functools.reduce(jnp.maximum, scores)
                top = jnp.max(top, axis=1, keepdims=True) * scale
                powers = [jnp.exp2(tile * scale - top) for tile in scores]
                total = jnp.sum(functools.reduce(jnp.add, powers), axis=1, keepdims=True)
                weights = jnp.concatenate([p.astype(jnp.bfloat16) for p in powers], axis=1)
                values = jnp.concatenate([kv_ref[0, spot, 1] for spot in spots], axis=0)
                result = jnp.dot(weights, values, preferred_element_type=jnp.float32)
                result = (result / total).astype(jnp.bfloat16)
                for h in range(group_size):
                    out_ref[pl.ds(start, BLOCK), h * head_dim : (h + 1) * head_dim] = result[
                        h * BLOCK : (h + 1) * BLOCK
                    ]

        return carry

    lax.fori_loop(0, per_dev, one_block, 0)


def attend(queries, tiles, vert_blocks, vert_count, slash_offsets, slash_count, device, group_size):
    rows_dev = queries.shape[0]
    kv_heads, n_tiles, _, _, head_dim = tiles.shape
    n_vert = vert_blocks.shape[1]
    n_slash = slash_offsets.shape[1]
    per_dev = rows_dev // BLOCK
    width = group_size * head_dim
    dims = (per_dev, n_vert, n_slash, group_size, head_dim)
    pairs = kv_heads * group_size * rows_dev * (n_vert + n_slash) * BLOCK
    return pl.pallas_call(
        functools.partial(attend_kernel, dims),
        out_shape=jax.ShapeDtypeStruct(queries.shape, jnp.bfloat16),
        grid_spec=pltpu.PrefetchScalarGridSpec(
            num_scalar_prefetch=5,
            grid=(kv_heads,),
            in_specs=[
                pl.BlockSpec((rows_dev, width), lambda g, *_: (0, g)),
                pl.BlockSpec((1, n_tiles, 2, BLOCK, head_dim), lambda g, *_: (g, 0, 0, 0, 0)),
            ],
            out_specs=pl.BlockSpec((rows_dev, width), lambda g, *_: (0, g)),
            scratch_shapes=[pltpu.SMEM((n_vert + n_slash,), jnp.int32)],
        ),
        compiler_params=pltpu.CompilerParams(
            dimension_semantics=("arbitrary",), vmem_limit_bytes=48 * 1024 * 1024
        ),
        cost_estimate=pl.CostEstimate(
            flops=4 * pairs * head_dim, bytes_accessed=4 * queries.size, transcendentals=pairs
        ),
        name="attend",
    )(vert_blocks, vert_count, slash_offsets, slash_count, device, queries, tiles)


def spread_kernel(
    dims, own_ref, term_ref, out_ref, acc, landed, full,
    far_send, far_recv, near_send, near_recv, fold_send, fold_recv, grow_send, grow_recv, keep_sem,
):
    size, kv_heads, own_rows, col_rows = dims
    head_rows = (REACH + 1) * own_rows + col_rows
    rounds = size.bit_length() - 1
    device = lax.axis_index("ctx")
    odd = lax.rem(device, 2)
    sends_far = device < size - REACH
    gets_far = device >= REACH
    gets_near = device >= 1
    partners = []
    bits = []
    for k in range(rounds):
        bit = lax.rem(device // (1 << k), 2)
        bits.append(bit)
        partners.append(device + (1 << k) * (1 - 2 * bit))

    def remote(src, dst, send, recv, target):
        return pltpu.make_async_remote_copy(
            src_ref=src, dst_ref=dst, send_sem=send, recv_sem=recv,
            device_id={"ctx": target}, device_id_type=pl.DeviceIdType.MESH,
        )

    def out_rows(head, place, rows):
        return out_ref.at[pl.ds(head * head_rows + place * own_rows, rows)]

    def far_copy(head):
        src = own_ref.at[pl.ds(head * own_rows, own_rows)]
        target = jnp.minimum(device + REACH, size - 1)
        return remote(src, out_rows(head, 0, own_rows), far_send.at[head], far_recv.at[head], target)

    def near_copy(head):
        src = own_ref.at[pl.ds(head * own_rows, own_rows)]
        return remote(
            src, out_rows(head, 1, own_rows), near_send.at[head], near_recv.at[head], partners[0]
        )

    def relay_copy(head):
        return remote(
            out_rows(head, 0, own_rows), out_rows(head, 1, own_rows),
            near_send.at[head], near_recv.at[head], partners[0],
        )

    barrier = pltpu.get_barrier_semaphore()
    for partner in partners:
        pl.semaphore_signal(
            barrier, inc=1, device_id={"ctx": partner}, device_id_type=pl.DeviceIdType.MESH
        )

    @pl.when(sends_far)
    def _():
        pl.semaphore_signal(
            barrier, inc=1, device_id={"ctx": device + REACH}, device_id_type=pl.DeviceIdType.MESH
        )

    @pl.when(gets_far)
    def _():
        pl.semaphore_signal(
            barrier, inc=1, device_id={"ctx": device - REACH}, device_id_type=pl.DeviceIdType.MESH
        )

    arrivals = rounds + sends_far.astype(jnp.int32) + gets_far.astype(jnp.int32)
    pl.semaphore_wait(barrier, arrivals)

    def start_far(heads):
        @pl.when(sends_far)
        def _():
            for head in heads:
                far_copy(head).start()

    early = range(kv_heads // 2)
    late = range(kv_heads // 2, kv_heads)
    base = jnp.int32(0)
    length = kv_heads * col_rows
    offset = 0
    bases = []
    folds = []
    for k in range(rounds):
        half = length // 2
        kept = pl.multiple_of(base + bits[k] * half, 16)
        given = pl.multiple_of(base + (1 - bits[k]) * half, 16)
        source = term_ref if k == 0 else acc
        copy = remote(
            source.at[pl.ds(given, half)], landed.at[pl.ds(offset, half)],
            fold_send.at[k], fold_recv.at[k], partners[k],
        )
        copy.start()
        folds.append(copy)
        if k == min(1, rounds - 1):
            start_far(early)
            for head in range(kv_heads):
                pltpu.make_async_copy(
                    own_ref.at[pl.ds(head * own_rows, own_rows)],
                    out_rows(head, REACH, own_rows), keep_sem.at[head],
                ).start()

            @pl.when(odd == 0)
            def _():
                for head in range(kv_heads):
                    near_copy(head).start()

        copy.wait_recv()
        step = min(half, 256)

        def add(i, carry, kept=kept, offset=offset, source=source, step=step, k=k):
            here = pl.ds(pl.multiple_of(kept + i * step, 16), step)
            there = pl.ds(pl.multiple_of(offset + i * step, 16), step)
            total = source[here, :] + landed[there, :]
            if k == rounds - 1:
                full[here, :] = total
            else:
                acc[here, :] = total
            return carry

        lax.fori_loop(0, half // step, add, 0)
        bases.append(kept)
        base, length, offset = kept, half, offset + half

    grows = []
    for k in reversed(range(rounds)):
        part = pl.ds(bases[k], (kv_heads * col_rows) >> (k + 1))
        copy = remote(full.at[part], full.at[part], grow_send.at[k], grow_recv.at[k], partners[k])
        copy.start()
        grows.append(copy)
        if k == min(1, rounds - 1):
            start_far(late)
        copy.wait_recv()

    cols = []
    for head in range(kv_heads):
        copy = pltpu.make_async_copy(
            full.at[pl.ds(head * col_rows, col_rows)],
            out_rows(head, REACH + 1, col_rows), keep_sem.at[kv_heads + head],
        )
        copy.start()
        cols.append(copy)

    @pl.when(gets_far)
    def _():
        for head in range(kv_heads):
            far_copy(head).wait_recv()

            @pl.when(odd == 1)
            def _(head=head):
                relay_copy(head).start()

    @pl.when((odd == 1) | gets_far)
    def _():
        for head in range(kv_heads):
            near_copy(head).wait_recv()

    @pl.when((odd == 0) | gets_far)
    def _():
        for head in range(kv_heads):
            near_copy(head).wait_send()

    @pl.when(sends_far)
    def _():
        for head in range(kv_heads):
            far_copy(head).wait_send()

    for copy in folds + grows:
        copy.wait_send()
    for head in range(kv_heads):
        pltpu.make_async_copy(
            own_ref.at[pl.ds(head * own_rows, own_rows)],
            out_rows(head, REACH, own_rows), keep_sem.at[head],
        ).wait()
    for copy in cols:
        copy.wait()


def spread(own, term):
    size = lax.axis_size("ctx")
    kv_heads, per_dev, _, _, head_dim = own.shape
    n_vert = term.shape[1]
    own_rows = per_dev * 2 * BLOCK
    col_rows = n_vert * 2 * BLOCK
    n_tiles = (REACH + 1) * per_dev + n_vert
    dims = (size, kv_heads, own_rows, col_rows)
    rounds = size.bit_length() - 1
    dma = pltpu.SemaphoreType.DMA
    columns = pltpu.VMEM((kv_heads * col_rows, head_dim), own.dtype)
    out = pl.pallas_call(
        functools.partial(spread_kernel, dims),
        out_shape=jax.ShapeDtypeStruct((kv_heads * n_tiles * 2 * BLOCK, head_dim), own.dtype),
        in_specs=[pl.BlockSpec(memory_space=pltpu.VMEM)] * 2,
        out_specs=pl.BlockSpec(memory_space=pl.ANY),
        scratch_shapes=[columns, columns, columns]
        + [dma((kv_heads,))] * 4
        + [dma((rounds,))] * 4
        + [dma((2 * kv_heads,))],
        compiler_params=pltpu.CompilerParams(
            collective_id=0, has_side_effects=True, vmem_limit_bytes=48 * 1024 * 1024
        ),
        name="spread",
    )(own.reshape(-1, head_dim), term.reshape(-1, head_dim))
    return out.reshape(kv_heads, n_tiles, 2, BLOCK, head_dim)


def local(
    query_states, key_states, value_states, vert_blocks, vert_count, slash_offsets, slash_count
):
    rows_dev, q_heads, head_dim = query_states.shape
    kv_heads = key_states.shape[1]
    group_size = q_heads // kv_heads
    per_dev = rows_dev // BLOCK
    n_vert = vert_blocks.shape[1]
    device = lax.axis_index("ctx")

    def by_tile(x):
        return jnp.transpose(x.reshape(per_dev, BLOCK, kv_heads, head_dim), (2, 0, 1, 3))

    own = jnp.stack((by_tile(key_states), by_tile(value_states)), axis=2)
    local_block = vert_blocks - device * per_dev
    used_slot = jnp.arange(n_vert)[None, :] < vert_count[:, None]
    mine = used_slot & (local_block >= 0) & (local_block < per_dev)
    term = jnp.take_along_axis(
        own, jnp.clip(local_block, 0, per_dev - 1)[:, :, None, None, None], axis=1
    )
    term = jnp.where(mine[:, :, None, None, None], term, jnp.bfloat16(0))
    tiles = spread(own, term)
    out = attend(
        query_states.reshape(rows_dev, q_heads * head_dim),
        tiles,
        vert_blocks,
        vert_count,
        slash_offsets,
        slash_count,
        device.reshape(1).astype(jnp.int32),
        group_size,
    )
    return out.reshape(rows_dev, q_heads, head_dim)


def solution(mesh):
    in_specs = (
        P(("groups", "ctx"), None, None),
        P(("groups", "ctx"), None, None),
        P(("groups", "ctx"), None, None),
        P("groups", None),
        P("groups"),
        P("groups", None),
        P("groups"),
    )
    out_specs = P(("groups", "ctx"), None, None)
    return jax.shard_map(local, mesh=mesh, in_specs=in_specs, out_specs=out_specs, check_vma=False)
```

profile of v0, /device:TPU:15, one launch (start us, length us, event | category | flops | bytes accessed | tf_op | source)
XLA Modules:
  0.0 158.0 jit_solution(11401884357246834658)
XLA Ops:
  0.0 0.7 fusion.2
  0.7 0.1 copy.17
  0.8 0.1 copy.18
  0.9 0.7 bitcast_or_fusion
  1.6 0.1 copy.19
  1.7 0.1 reshape.55
  1.7 0.8 copy.21.so_ref
  2.5 0.8 copy.20.vb_ref
  3.3 0.1 broadcast_in_dim.35
  3.4 0.1 broadcast_in_dim.32
  3.5 2.1 %copy_bitcast_fusion.1 = (bf16[8,4,1,128,128]{4,3,2,1,0:T(8,128)(2,1)S(1)}, bf16[8,4,1,128,128]{4,3,2,1,0:T(8,128)(2,1)S(1)}) fusion(bf16[4,128,8,128]{3,2,1,0:T(8,128)(2,1)} %bitcast.32, bf16[4,128,8,128]{3,2,1,0:T(8,128)(2,1)} %bitcast.33), kind=kLoop, calls=%fused_computation.5 | loop fusion | bytes 4194304 | tf_op jit(solution)/shard_map/stack | solution.py:329
  5.6 0.2 pad_maximum_fusion
  5.8 2.1 %gather_fusion = bf16[32,2,128,128]{3,2,1,0:T(8,128)(2,1)} fusion(bf16[8,4,2,128,128]{4,3,2,1,0:T(8,128)(2,1)S(1)} %pad_maximum_fusion, s32[32]{0:T(128)S(1)} %reshape.55), kind=kCustom, calls=%fused_computation | custom fusion | bytes 4194560 | tf_op jit(solution)/shard_map/jit(take_along_axis)/gather | solution.py:333
  8.0 7.0 %fusion.term_ref = bf16[8192,128]{1,0:T(8,128)(2,1)S(1)} fusion(bf16[32,2,128,128]{3,2,1,0:T(8,128)(2,1)} %gather_fusion, pred[8192]{0:T(1024)(128)(4,1)S(1)} %broadcast_in_dim.36, pred[8192]{0:T(1024)(128)(4,1)S(1)} %broadcast_in_dim.33), kind=kLoop, calls=%fused_computation.4 | loop fusion | flops 2097152 | bytes 4210688 | tf_op jit(solution)/shard_map/jit(_where)/select_n | solution.py:336
  14.9 0.0 copy-start.2
  15.0 105.4 %spread.1 = bf16[32768,128]{1,0:T(8,128)(2,1)} custom-call(bf16[8192,128]{1,0:T(8,128)(2,1)S(1)} %bitcast.27, bf16[8192,128]{1,0:T(8,128)(2,1)S(1)} %fusion.term_ref), custom_call_target="tpu_custom_call" | custom-call | tf_op jit(solution)/shard_map/spread/pallas_call | solution.py:299
  120.4 0.0 copy-done.2
  120.4 0.0 copy-start
  120.4 0.0 copy-start.1
  120.4 6.2 %copy.27 = bf16[64,8,32,128]{3,1,2,0:T(8,128)(2,1)} copy(bf16[64,8,32,128]{3,2,1,0:T(8,128)(2,1)S(1)} %bitcast.30) | data formatting | bytes 8388608
  126.6 0.0 copy-done
  126.6 0.0 copy-done.1
  126.6 28.1 %attend.1 = bf16[512,4096]{1,0:T(8,128)(2,1)S(1)} custom-call(s32[8,4]{1,0:T(8,128)S(1)} %copy.20.vb_ref, s32[8]{0:T(128)S(1)} %copy-done, s32[8,4]{1,0:T(8,128)S(1)} %copy.21.so_ref, s32[8]{0:T(128)S(1)} %copy-done.1, s32[1]{0:T(128)} %bitcast.dev_ref, bf16[512,4096]{1,0:T(8,128)(2,1)} %bitcast.31, bf16[8,16,2,128,128]{4,3,2,1,0:T(8,128)(2,1)} %bitcast.29), custom_call_target="tpu_custom_call" | custom-call | flops 8589934592 | bytes 8388608 | tf_op jit(solution)/shard_map/attend/pallas_call | solution.py:91
  154.7 3.3 %copy.23 = bf16[64,8,32,128]{3,2,1,0:T(8,128)(2,1)} copy(bf16[64,8,32,128]{3,1,2,0:T(8,128)(2,1)S(1)} %bitcast.28) | data formatting | bytes 8388608
  (2 shorter events, 0.1 us)
Async XLA Ops:
  14.9 105.4 %copy-start.2 = (bf16[512,32,128]{2,1,0:T(8,128)(2,1)S(1)}, bf16[512,32,128]{2,1,0:T(8,128)(2,1)}, u32[]{:S(2)}) copy-start(bf16[512,32,128]{2,1,0:T(8,128)(2,1)} %param.7) | copy-start | bytes 12582916
  120.4 6.2 %copy-start = (s32[8]{0:T(128)S(1)}, s32[8]{0:T(128)}, u32[]{:S(2)}) copy-start(s32[8]{0:T(128)} %vc_ref.1) | copy-start | bytes 100
  120.4 6.2 %copy-start.1 = (s32[8]{0:T(128)S(1)}, s32[8]{0:T(128)}, u32[]{:S(2)}) copy-start(s32[8]{0:T(128)} %sc_ref.1) | copy-start | bytes 100
where the time goes:
time: 159 us; the launch traced here: 158 us
  Pallas kernels  134 us (84%)
  local copies, waits for them, and re-layouts  15.8 us (10%)
  other arithmetic  8.57 us (5%)
    pallas_call x1, Pallas kernels, spread(): pl.pallas_call(functools.partial(spread_kernel, dims), out_shape=jax.Shap...  105 us
    pallas_call x1, Pallas kernels, attend(): pl.pallas_call(functools.partial(attend_kernel, dims), out_shape=jax.Shap...  28.1 us
    unnamed x10, local copies, waits for them, and re-layouts  11 us
    select_n x1, other arithmetic, local(): term = jnp.where(mine[:, :, None, None, None], term, jnp.bfloat16(0))  6.98 us

commit v1 on v0

v1 whole, which is shorter than its diff:
```python
import functools
import math

import jax
import jax.numpy as jnp
from jax import lax
from jax.experimental import pallas as pl
from jax.experimental.pallas import tpu as pltpu
from jax.sharding import PartitionSpec as P

BLOCK = 128
LARGEST_OFFSET = 8
MASKED = -1e30


def attend_head(head, dims, device, tables, q_ref, window, columns, diagonal, unit, out_ref):
    per_dev, reach, n_vert, n_slash, group_size, head_dim = dims
    vb_ref, vc_ref, so_ref, sc_ref = tables
    scale = math.log2(math.e) / math.sqrt(head_dim)
    n_tiles = n_vert + n_slash
    chunk = 2 if group_size % 2 == 0 else 1
    parts = group_size // chunk

    def one_block(block, carry):
        qblock = device * per_dev + block
        start = pl.multiple_of(block * BLOCK, BLOCK)
        own = reach * per_dev + block
        spots, usable = [own], []
        for s in range(1, n_slash):
            offset = so_ref[head, s]
            ok = (s < sc_ref[head]) & (offset <= qblock)
            for v in range(n_vert):
                ok = ok & ((v >= vc_ref[head]) | (vb_ref[head, v] != qblock - offset))
            usable.append(ok)
            spots.append(jnp.where(ok, own - offset, own))
        for v in range(n_vert):
            usable.append((v < vc_ref[head]) & (vb_ref[head, v] < qblock))
        keys = [window[spot, 0] for spot in spots]
        values = [window[spot, 1] for spot in spots]
        for v in range(n_vert):
            row = (head * n_vert + v) * 2 * BLOCK
            keys.append(columns[row : row + BLOCK, :])
            values.append(columns[row + BLOCK : row + 2 * BLOCK, :])
        masks = [diagonal[...]]
        for ok in usable:
            fill = jnp.where(ok, 0.0, MASKED).astype(jnp.float32)
            masks.append(jnp.full((BLOCK, BLOCK), fill, jnp.float32).astype(jnp.bfloat16))
        keys = jnp.concatenate(
            [jnp.concatenate(keys, axis=0), jnp.concatenate(masks, axis=0)], axis=1
        )
        ones = jnp.ones((n_tiles * BLOCK, head_dim), jnp.bfloat16)
        values = jnp.concatenate([jnp.concatenate(values, axis=0), ones], axis=1)

        def scores_of(part):
            queries = []
            for h in range(part * chunk, (part + 1) * chunk):
                lane = (head * group_size + h) * head_dim
                rows = q_ref[pl.ds(start, BLOCK), lane : lane + head_dim]
                queries.append(jnp.concatenate([rows, unit[...]], axis=1))
            tile = lax.dot_general(
                jnp.concatenate(queries, axis=0), keys, (((1,), (1,)), ((), ())),
                preferred_element_type=jnp.float32,
            )
            return [tile[:, i * BLOCK : (i + 1) * BLOCK] for i in range(n_tiles)]

        def top_of(scores):
            return jnp.max(functools.reduce(jnp.maximum, scores), axis=1, keepdims=True) * scale

        def sums_of(scores, top):
            powers = [jnp.exp2(tile * scale - top).astype(jnp.bfloat16) for tile in scores]
            return jnp.dot(
                jnp.concatenate(powers, axis=1), values, preferred_element_type=jnp.float32
            )

        def store(part, sums):
            result = (sums[:, :head_dim] / sums[:, head_dim:]).astype(jnp.bfloat16)
            for i in range(chunk):
                lane = (head * group_size + part * chunk + i) * head_dim
                out_ref[pl.ds(start, BLOCK), lane : lane + head_dim] = result[
                    i * BLOCK : (i + 1) * BLOCK
                ]

        scores = scores_of(0)
        top = top_of(scores)
        last = None
        for part in range(parts):
            following = scores_of(part + 1) if part + 1 < parts else None
            sums = sums_of(scores, top)
            if following is not None:
                top = top_of(following)
            if last is not None:
                store(part - 1, last)
            scores, last = following, sums
        store(parts - 1, last)
        return carry

    lax.fori_loop(0, per_dev, one_block, 0)


def fused_kernel(
    size, kv_heads, relayed, dims,
    vb_ref, vc_ref, so_ref, sc_ref, own_ref, q_ref, out_ref,
    acc, landed, full, stage, diagonal, unit, *scratch,
):
    per_dev, reach, n_vert, n_slash, group_size, head_dim = dims
    windows = scratch[:kv_heads]
    (
        fold_send, fold_recv, grow_send, grow_recv, far_send, far_recv,
        near_send, near_recv, pass_send, pass_recv,
    ) = scratch[kv_heads:]
    tables = (vb_ref, vc_ref, so_ref, sc_ref)
    device = lax.axis_index("ctx")
    odd = lax.rem(device, 2)
    side = lax.rem(device // 2, 2)
    line = device // 4
    line_bits = size.bit_length() - 3
    direct = kv_heads - relayed

    def remote(src, dst, send, recv, target):
        return pltpu.make_async_remote_copy(
            src_ref=src, dst_ref=dst, send_sem=send, recv_sem=recv,
            device_id={"ctx": target}, device_id_type=pl.DeviceIdType.MESH,
        )

    def when(condition):
        return pl.when(condition)

    last = size - 1
    sends_far = device + reach < size
    gets_far = device >= reach
    crossing = (side == 1) & sends_far
    passes = (side == 0) & (device + 2 * reach < size)
    gets_passed = (side == 0) & gets_far
    partner = device + 1 - 2 * odd

    masks, bits = [], []
    gray = line ^ (line // 2)
    for j in range(line_bits):
        k, r = j, line_bits - 1 - j
        masks.append(jnp.where(odd == 0, 4 * ((2 << k) - 1), 4 * ((2 << r) - 1)))
        bits.append(jnp.where(odd == 0, lax.rem(gray // (1 << k), 2), lax.rem(gray // (1 << r), 2)))
    partners = [partner] + [device ^ mask for mask in masks]
    bits = [odd] + bits
    across = device ^ 2
    rounds = len(partners)

    barrier = pltpu.get_barrier_semaphore()

    def greet(target):
        pl.semaphore_signal(
            barrier, inc=1, device_id={"ctx": target}, device_id_type=pl.DeviceIdType.MESH
        )

    for target in partners + [across]:
        greet(target)
    for condition, target in (
        (crossing, device + reach), (gets_passed, device - reach),
        (passes, device + 2 * reach), (gets_passed & (device >= 2 * reach), device - 2 * reach),
    ):
        @when(condition)
        def _(target=target):
            greet(target)

    rows_i = lax.broadcasted_iota(jnp.int32, (BLOCK, BLOCK), 0)
    cols_i = lax.broadcasted_iota(jnp.int32, (BLOCK, BLOCK), 1)
    diagonal[...] = jnp.where(cols_i >= rows_i, 0.0, MASKED).astype(jnp.bfloat16)
    unit[...] = jnp.where(rows_i == cols_i, 1.0, 0.0).astype(jnp.bfloat16)

    def one_head(head, carry):
        for v in range(n_vert):
            at = vb_ref[head, v] - device * per_dev
            mine = (v < vc_ref[head]) & (at >= 0) & (at < per_dev)
            at = jnp.clip(at, 0, per_dev - 1)
            for kv in range(2):
                tile = own_ref[head, at, kv].astype(jnp.float32)
                row = pl.multiple_of(((head * n_vert + v) * 2 + kv) * BLOCK, BLOCK)
                acc[pl.ds(row, BLOCK), :] = jnp.where(mine, tile, 0.0).astype(jnp.bfloat16)
        return carry

    lax.fori_loop(0, kv_heads, one_head, 0)
    for head in range(kv_heads):
        windows[head][reach * per_dev : (reach + 1) * per_dev] = own_ref[head]

    arrivals = jnp.int32(rounds + 1)
    for condition in (crossing, gets_passed, passes, gets_passed & (device >= 2 * reach)):
        arrivals = arrivals + condition.astype(jnp.int32)
    pl.semaphore_wait(barrier, arrivals)

    def place(head, where):
        return windows[head].at[pl.ds(where * per_dev, per_dev)]

    def far_copy(head):
        target = jnp.minimum(device + reach, last)
        return remote(own_ref.at[head], place(head, 0), far_send.at[head], far_recv.at[head], target)

    def stage_copy(head):
        slot = stage.at[head - direct]
        target = jnp.maximum(device - reach, 0)
        return remote(own_ref.at[head], slot, far_send.at[head], pass_recv.at[head - direct], target)

    def pass_copy(head):
        slot = stage.at[head - direct]
        target = jnp.minimum(device + 2 * reach, last)
        return remote(
            slot, place(head, 0), pass_send.at[head - direct], far_recv.at[head], target
        )

    def near_copy(head):
        return remote(
            own_ref.at[head], place(head, 1), near_send.at[head], near_recv.at[head], partner
        )

    def relay_copy(head):
        return remote(
            place(head, 0), place(head, 1), near_send.at[head], near_recv.at[head], partner
        )

    def start_far(condition, heads):
        @when(condition)
        def _():
            for head in heads:
                far_copy(head).start()

    total_rows = kv_heads * n_vert * 2 * BLOCK
    base, length, offset = jnp.int32(0), total_rows, 0
    bases, folds = [], []

    def fold(k):
        half = length // 2
        kept = pl.multiple_of(base + bits[k] * half, 16)
        given = pl.multiple_of(base + (1 - bits[k]) * half, 16)
        copy = remote(
            acc.at[pl.ds(given, half)], landed.at[pl.ds(offset, half)],
            fold_send.at[k], fold_recv.at[k], partners[k],
        )
        copy.start()
        return copy, kept, half

    def add(dst, kept, offset, rows):
        step = min(rows, 256)

        def body(i, carry):
            here = pl.ds(pl.multiple_of(kept + i * step, 16), step)
            there = pl.ds(pl.multiple_of(offset + i * step, 16), step)
            dst[here, :] = acc[here, :] + landed[there, :]
            return carry

        lax.fori_loop(0, rows // step, body, 0)

    early = 3 * kv_heads // 8
    for k in range(rounds):
        copy, kept, half = fold(k)
        folds.append(copy)
        if k == 0:
            start_far(side == 0, range(early))

            @when(crossing)
            def _():
                for head in range(direct, kv_heads):
                    stage_copy(head).start()

            @when(odd == 0)
            def _():
                for head in range(kv_heads):
                    near_copy(head).start()

        if k == rounds - 1:
            start_far(crossing, range(min(2, direct)))
        copy.wait_recv()
        add(acc, kept, offset, half)
        bases.append(kept)
        base, length, offset = kept, half, offset + half

    swap = remote(
        acc.at[pl.ds(base, length)], landed.at[pl.ds(offset, length)],
        fold_send.at[rounds], fold_recv.at[rounds], across,
    )
    swap.start()
    start_far(side == 0, range(early, kv_heads))
    swap.wait_recv()
    add(full, base, offset, length)
    folds.append(swap)

    grows = []
    for k in reversed(range(rounds)):
        part = pl.ds(bases[k], total_rows >> (k + 1))
        copy = remote(full.at[part], full.at[part], grow_send.at[k], grow_recv.at[k], partners[k])
        copy.start()
        grows.append(copy)
        if k == min(1, rounds - 1):
            start_far(crossing, range(min(2, direct), direct))

            @when(passes)
            def _():
                for head in range(direct, kv_heads):
                    stage_copy(head).wait_recv()
                    pass_copy(head).start()

        copy.wait_recv()

    for head in range(kv_heads):
        @when(gets_far)
        def _():
            far_copy(head).wait_recv()

            @when(odd == 1)
            def _():
                relay_copy(head).start()

        @when((odd == 1) | gets_far)
        def _():
            near_copy(head).wait_recv()

        attend_head(
            head, dims, device, tables, q_ref, windows[head], full, diagonal, unit, out_ref
        )

    @when(sends_far)
    def _():
        for head in range(kv_heads):
            far_copy(head).wait_send()

    @when((odd == 0) | gets_far)
    def _():
        for head in range(kv_heads):
            near_copy(head).wait_send()

    @when(passes)
    def _():
        for head in range(direct, kv_heads):
            pass_copy(head).wait_send()

    for copy in folds + grows:
        copy.wait_send()


def fused(own, queries, vert_blocks, vert_count, slash_offsets, slash_count, group_size):
    size = lax.axis_size("ctx")
    kv_heads, per_dev, _, _, head_dim = own.shape
    n_vert = vert_blocks.shape[1]
    n_slash = slash_offsets.shape[1]
    reach = -(-LARGEST_OFFSET // per_dev)
    relayed = 3 * kv_heads // 8
    rounds = size.bit_length() - 2
    dims = (per_dev, reach, n_vert, n_slash, group_size, head_dim)
    dma = pltpu.SemaphoreType.DMA
    columns = pltpu.VMEM((kv_heads * n_vert * 2 * BLOCK, head_dim), own.dtype)
    square = pltpu.VMEM((BLOCK, BLOCK), own.dtype)
    window = pltpu.VMEM(((reach + 1) * per_dev, 2, BLOCK, head_dim), own.dtype)
    smem = pl.BlockSpec(memory_space=pltpu.SMEM)
    vmem = pl.BlockSpec(memory_space=pltpu.VMEM)
    return pl.pallas_call(
        functools.partial(fused_kernel, size, kv_heads, relayed, dims),
        out_shape=jax.ShapeDtypeStruct(queries.shape, queries.dtype),
        in_specs=[smem] * 4 + [vmem] * 2,
        out_specs=vmem,
        scratch_shapes=[columns] * 3
        + [pltpu.VMEM((relayed, per_dev, 2, BLOCK, head_dim), own.dtype)]
        + [square] * 2
        + [window] * kv_heads
        + [dma((rounds + 1,))] * 2
        + [dma((rounds,))] * 2
        + [dma((kv_heads,))] * 4
        + [dma((relayed,))] * 2,
        compiler_params=pltpu.CompilerParams(
            collective_id=0, has_side_effects=True, vmem_limit_bytes=56 * 1024 * 1024
        ),
        name="fused",
    )(vert_blocks, vert_count, slash_offsets, slash_count, own, queries)


def local(
    query_states, key_states, value_states, vert_blocks, vert_count, slash_offsets, slash_count
):
    rows_dev, q_heads, head_dim = query_states.shape
    kv_heads = key_states.shape[1]
    group_size = q_heads // kv_heads
    per_dev = rows_dev // BLOCK

    def by_tile(x):
        return jnp.transpose(x.reshape(per_dev, BLOCK, kv_heads, head_dim), (2, 0, 1, 3))

    own = jnp.stack((by_tile(key_states), by_tile(value_states)), axis=2)
    out = fused(
        own,
        query_states.reshape(rows_dev, q_heads * head_dim),
        vert_blocks,
        vert_count,
        slash_offsets,
        slash_count,
        group_size,
    )
    return out.reshape(rows_dev, q_heads, head_dim)


def solution(mesh):
    in_specs = (
        P(("groups", "ctx"), None, None),
        P(("groups", "ctx"), None, None),
        P(("groups", "ctx"), None, None),
        P("groups", None),
        P("groups"),
        P("groups", None),
        P("groups"),
    )
    out_specs = P(("groups", "ctx"), None, None)
    return jax.shard_map(local, mesh=mesh, in_specs=in_specs, out_specs=out_specs, check_vma=False)
```

time: 159 us -> 129 us (0.81)
  the two profiles are of different devices: /device:TPU:15 before, /device:TPU:24 now
where the time goes in v1:
time: 129 us; the launch traced here: 128 us
  Pallas kernels  110 us (85%)
  local copies, waits for them, and re-layouts  17.3 us (13%)
  other arithmetic  1.51 us (1%)
    pallas_call x1, Pallas kernels, fused(): pl.pallas_call(functools.partial(fused_kernel, size, kv_heads, relayed, d...  110 us
    unnamed x8, local copies, waits for them, and re-layouts  17.3 us

profile of v1, /device:TPU:24, one launch (start us, length us, event | category | flops | bytes accessed | tf_op | source)
XLA Modules:
  0.0 128.4 jit_solution(8238347492322329192)
XLA Ops:
  0.0 1.3 %copy.10.vb_ref = s32[8,4]{1,0:T(8,128)} copy(s32[8,4]{0,1:T(4,128)} %param.10) | data formatting | bytes 256 | tf_op args[3]
  1.3 1.3 %copy.11.so_ref = s32[8,4]{1,0:T(8,128)} copy(s32[8,4]{0,1:T(4,128)} %param.12) | data formatting | bytes 256 | tf_op args[5]
  2.7 0.0 copy-start
  2.7 1.5 %copy.8 = bf16[512,8,128]{2,0,1:T(8,128)(2,1)S(1)} copy(bf16[512,8,128]{2,1,0:T(8,128)(2,1)} %param.8) | data formatting | bytes 2097152 | tf_op args[1]
  4.2 1.4 %copy.9 = bf16[512,8,128]{2,0,1:T(8,128)(2,1)S(1)} copy(bf16[512,8,128]{2,1,0:T(8,128)(2,1)} %param.9) | data formatting | bytes 2097152 | tf_op args[2]
  5.6 1.5 %pad_maximum_fusion.own_ref = bf16[8,4,2,128,128]{4,3,2,1,0:T(8,128)(2,1)} fusion(bf16[8,4,1,128,128]{4,3,2,1,0:T(8,128)(2,1)S(1)} %bitcast.20, bf16[8,4,1,128,128]{4,3,2,1,0:T(8,128)(2,1)S(1)} %bitcast.19), kind=kLoop, calls=%fused_computation.1 | loop fusion | flops 1048576 | bytes 4194304 | tf_op jit(solution)/shard_map/stack | solution.py:383
  7.1 0.0 copy-done
  7.1 6.2 %copy.15 = bf16[64,8,32,128]{3,1,2,0:T(8,128)(2,1)} copy(bf16[64,8,32,128]{3,2,1,0:T(8,128)(2,1)S(1)} %bitcast.18) | data formatting | bytes 8388608
  13.3 109.6 %fused.1 = bf16[512,4096]{1,0:T(8,128)(2,1)} custom-call(s32[8,4]{1,0:T(8,128)} %copy.10.vb_ref, s32[8]{0:T(128)} %vc_ref.1, s32[8,4]{1,0:T(8,128)} %copy.11.so_ref, s32[8]{0:T(128)} %sc_ref.1, bf16[8,4,2,128,128]{4,3,2,1,0:T(8,128)(2,1)} %pad_maximum_fusion.own_ref, bf16[512,4096]{1,0:T(8,128)(2,1)} %bitcast.17), custom_call_target="tpu_custom_call" | custom-call | tf_op jit(solution)/shard_map/fused/pallas_call | solution.py:352
  122.9 5.5 %copy.13 = bf16[64,8,32,128]{3,2,1,0:T(8,128)(2,1)} copy(bf16[64,8,32,128]{3,1,2,0:T(8,128)(2,1)} %bitcast.16) | data formatting | bytes 8388608
Async XLA Ops:
  2.7 4.5 %copy-start = (bf16[512,32,128]{2,1,0:T(8,128)(2,1)S(1)}, bf16[512,32,128]{2,1,0:T(8,128)(2,1)}, u32[]{:S(2)}) copy-start(bf16[512,32,128]{2,1,0:T(8,128)(2,1)} %param.7) | copy-start | bytes 12582916

commit v2 on v1

v2 whole, which is shorter than its diff:
```python
import functools
import math

import jax
import jax.numpy as jnp
from jax import lax
from jax.experimental import pallas as pl
from jax.experimental.pallas import tpu as pltpu
from jax.sharding import PartitionSpec as P

BLOCK = 128
LARGEST_OFFSET = 8
MASKED = -1e30
CHUNKS = 2


def attend_head(head, dims, device, tables, q_ref, window, columns, diagonal, unit, out_ref):
    per_dev, reach, n_vert, n_slash, group_size, head_dim = dims
    vb_ref, vc_ref, so_ref, sc_ref = tables
    scale = math.log2(math.e) / math.sqrt(head_dim)
    n_tiles = n_vert + n_slash
    chunk = 2 if group_size % 2 == 0 else 1
    parts = group_size // chunk

    def one_block(block, carry):
        qblock = device * per_dev + block
        start = pl.multiple_of(block * BLOCK, BLOCK)
        own = reach * per_dev + block
        spots, usable = [own], []
        for s in range(1, n_slash):
            offset = so_ref[s, head]
            ok = (s < sc_ref[head]) & (offset <= qblock)
            for v in range(n_vert):
                ok = ok & ((v >= vc_ref[head]) | (vb_ref[v, head] != qblock - offset))
            usable.append(ok)
            spots.append(jnp.where(ok, own - offset, own))
        for v in range(n_vert):
            usable.append((v < vc_ref[head]) & (vb_ref[v, head] < qblock))
        keys = [window[spot, 0] for spot in spots]
        values = [window[spot, 1] for spot in spots]
        for v in range(n_vert):
            row = (head * n_vert + v) * 2 * BLOCK
            keys.append(columns[row : row + BLOCK, :])
            values.append(columns[row + BLOCK : row + 2 * BLOCK, :])
        masks = [diagonal[...]]
        for ok in usable:
            fill = jnp.where(ok, 0.0, MASKED).astype(jnp.float32)
            masks.append(jnp.full((BLOCK, BLOCK), fill, jnp.float32).astype(jnp.bfloat16))
        keys = jnp.concatenate(
            [jnp.concatenate(keys, axis=0), jnp.concatenate(masks, axis=0)], axis=1
        )
        values = jnp.concatenate(values, axis=0)

        def scores_of(part):
            queries = []
            for h in range(part * chunk, (part + 1) * chunk):
                lane = (head * group_size + h) * head_dim
                rows = q_ref[pl.ds(start, BLOCK), lane : lane + head_dim]
                queries.append(jnp.concatenate([rows, unit[...]], axis=1))
            tile = lax.dot_general(
                jnp.concatenate(queries, axis=0), keys, (((1,), (1,)), ((), ())),
                preferred_element_type=jnp.float32,
            )
            return [tile[:, i * BLOCK : (i + 1) * BLOCK] for i in range(n_tiles)]

        def top_of(scores):
            return jnp.max(functools.reduce(jnp.maximum, scores), axis=1, keepdims=True)

        def sums_of(scores, top):
            powers = [jnp.exp2((tile - top) * scale) for tile in scores]
            total = jnp.sum(functools.reduce(jnp.add, powers), axis=1, keepdims=True)
            weights = jnp.concatenate([p.astype(jnp.bfloat16) for p in powers], axis=1)
            return jnp.dot(weights, values, preferred_element_type=jnp.float32), total

        def store(part, sums):
            result = (sums[0] / sums[1]).astype(jnp.bfloat16)
            for i in range(chunk):
                lane = (head * group_size + part * chunk + i) * head_dim
                out_ref[pl.ds(start, BLOCK), lane : lane + head_dim] = result[
                    i * BLOCK : (i + 1) * BLOCK
                ]

        scores = scores_of(0)
        top = top_of(scores)
        last = None
        for part in range(parts):
            following = scores_of(part + 1) if part + 1 < parts else None
            sums = sums_of(scores, top)
            if following is not None:
                top = top_of(following)
            if last is not None:
                store(part - 1, last)
            scores, last = following, sums
        store(parts - 1, last)
        return carry

    lax.fori_loop(0, per_dev, one_block, 0, unroll=2 if per_dev % 2 == 0 else 1)


def fused_kernel(
    size, kv_heads, relayed, dims,
    vb_ref, vc_ref, so_ref, sc_ref, k_ref, v_ref, q_ref, out_ref,
    own_ref, qs_ref, acc, landed, full, stage, diagonal, unit, *scratch,
):
    per_dev, reach, n_vert, n_slash, group_size, head_dim = dims
    windows = scratch[:kv_heads]
    (
        core_send, core_recv, grow_send, grow_recv, swap_send, swap_recv,
        up_recv, down_recv, line_send, spread_recv, above_send, below_send,
        far_send, far_recv, near_send, near_recv, pass_send, pass_recv,
    ) = scratch[kv_heads:]
    tables = (vb_ref, vc_ref, so_ref, sc_ref)
    device = lax.axis_index("ctx")
    odd = lax.rem(device, 2)
    side = lax.rem(device // 2, 2)
    line = device // 4
    length = size // 4
    direct = kv_heads - relayed
    last = size - 1

    def remote(src, dst, send, recv, target):
        return pltpu.make_async_remote_copy(
            src_ref=src, dst_ref=dst, send_sem=send, recv_sem=recv,
            device_id={"ctx": target}, device_id_type=pl.DeviceIdType.MESH,
        )

    sends_far = device + reach < size
    gets_far = device >= reach
    crossing = (side == 1) & sends_far
    passes = (side == 0) & (device + 2 * reach < size)
    gets_passed = (side == 0) & gets_far
    partner = device + 1 - 2 * odd
    across = device ^ 2
    above = jnp.minimum(device + 4, last)
    below = jnp.maximum(device - 4, 0)
    has_above = line < length - 1
    has_below = line > 0

    barrier = pltpu.get_barrier_semaphore()
    greeted = (
        (has_above, above), (has_below, below),
        (crossing, device + reach), (gets_passed, device - reach),
    )

    def greet(target):
        pl.semaphore_signal(
            barrier, inc=1, device_id={"ctx": target}, device_id_type=pl.DeviceIdType.MESH
        )

    greet(partner)
    greet(across)
    arrivals = jnp.int32(2)
    for condition, target in greeted:
        @pl.when(condition)
        def _(target=target):
            greet(target)

        arrivals = arrivals + condition.astype(jnp.int32)

    rows_i = lax.broadcasted_iota(jnp.int32, (BLOCK, BLOCK), 0)
    cols_i = lax.broadcasted_iota(jnp.int32, (BLOCK, BLOCK), 1)
    diagonal[...] = jnp.where(cols_i >= rows_i, 0.0, MASKED).astype(jnp.bfloat16)
    unit[...] = jnp.where(rows_i == cols_i, 1.0, 0.0).astype(jnp.bfloat16)

    def own_block(block, carry):
        rows = pl.ds(pl.multiple_of(block * BLOCK, BLOCK), BLOCK)
        for kv, ref in enumerate((k_ref, v_ref)):
            for head in range(kv_heads):
                tile = ref[rows, head, :]
                own_ref[head, block, kv] = tile
                windows[head][reach * per_dev + block, kv] = tile
        return carry

    with jax.named_scope("own"):
        lax.fori_loop(0, per_dev, own_block, 0)

    def one_head(head, carry):
        for v in range(n_vert):
            at = vb_ref[v, head] - device * per_dev
            mine = (v < vc_ref[head]) & (at >= 0) & (at < per_dev)
            at = jnp.clip(at, 0, per_dev - 1)
            for kv in range(2):
                tile = own_ref[head, at, kv].astype(jnp.float32)
                row = pl.multiple_of(((head * n_vert + v) * 2 + kv) * BLOCK, BLOCK)
                acc[pl.ds(row, BLOCK), :] = jnp.where(mine, tile, 0.0).astype(jnp.bfloat16)
        return carry

    with jax.named_scope("terms"):
        lax.fori_loop(0, kv_heads, one_head, 0)
    with jax.named_scope("entry"):
        pl.semaphore_wait(barrier, arrivals)

    def place(head, where):
        return windows[head].at[pl.ds(where * per_dev, per_dev)]

    def far_copy(head):
        target = jnp.minimum(device + reach, last)
        return remote(own_ref.at[head], place(head, 0), far_send.at[head], far_recv.at[head], target)

    def stage_copy(head):
        slot = stage.at[head - direct]
        target = jnp.maximum(device - reach, 0)
        return remote(own_ref.at[head], slot, far_send.at[head], pass_recv.at[head - direct], target)

    def pass_copy(head):
        slot = stage.at[head - direct]
        return remote(
            slot, place(head, 0), pass_send.at[head - direct], far_recv.at[head], above
        )

    def near_copy(head):
        return remote(
            own_ref.at[head], place(head, 1), near_send.at[head], near_recv.at[head], partner
        )

    def relay_copy(head):
        return remote(
            place(head, 0), place(head, 1), near_send.at[head], near_recv.at[head], partner
        )

    def start_far(condition, heads):
        @pl.when(condition)
        def _():
            for head in heads:
                far_copy(head).start()

    def pass_on(heads):
        @pl.when(passes)
        def _():
            for head in heads:
                with jax.named_scope(f"stage#h={head}"):
                    stage_copy(head).wait_recv()
                pass_copy(head).start()

    chunk_rows = kv_heads * n_vert * 2 * BLOCK // CHUNKS
    half = chunk_rows // 2
    piece = half // length
    chunks = range(CHUNKS)

    def kept(c):
        return c * chunk_rows + odd * half

    def part(c, d):
        return pl.ds(pl.multiple_of(kept(c) + d * piece, 16), piece)

    def spot(c, d, way):
        return pl.ds(pl.multiple_of(((c * length + d) * 2 + way) * piece, 16), piece)

    def add(dst, at, landing, rows):
        step = min(rows, 256)

        def body(i, carry):
            here = pl.ds(pl.multiple_of(at + i * step, 16), step)
            there = pl.ds(pl.multiple_of(landing + i * step, 16), step)
            dst[here, :] = acc[here, :] + landed[there, :]
            return carry

        lax.fori_loop(0, rows // step, body, 0)

    def core_copy(c):
        given = pl.multiple_of(c * chunk_rows + (1 - odd) * half, 16)
        return remote(
            acc.at[pl.ds(given, half)], landed.at[pl.ds(landed_core + c * half, half)],
            core_send.at[c], core_recv.at[c], partner,
        )

    landed_core = CHUNKS * length * 2 * piece
    landed_swap = landed_core + CHUNKS * half

    def line_copy(c, d, way):
        recv = up_recv if way == 0 else down_recv
        target = above if way == 0 else below
        return remote(
            acc.at[part(c, d)], landed.at[spot(c, d, way)],
            line_send.at[c, d], recv.at[c, d], target,
        )

    def take(c, d, way):
        line_copy(c, d, way).wait_recv()
        add(acc, kept(c) + d * piece, ((c * length + d) * 2 + way) * piece, piece)

    def fold_line(c):
        for d in range(length - 1, 0, -1):
            @pl.when(line < d)
            def _(d=d):
                @pl.when(has_below)
                def _():
                    take(c, d, 0)

                line_copy(c, d, 0).start()

        for d in range(length - 1):
            @pl.when(line > d)
            def _(d=d):
                @pl.when(has_above)
                def _():
                    take(c, d, 1)

                line_copy(c, d, 1).start()

    def finish_line(c):
        @pl.when(has_below)
        def _():
            take(c, line, 0)

        @pl.when(has_above)
        def _():
            take(c, line, 1)

    def swap_copy(c):
        return remote(
            acc.at[part(c, line)], landed.at[pl.ds(landed_swap + c * piece, piece)],
            swap_send.at[c], swap_recv.at[c], across,
        )

    def spread_copy(c, d, way):
        send = above_send if way == 0 else below_send
        target = above if way == 0 else below
        return remote(
            full.at[part(c, d)], full.at[part(c, d)], send.at[c, d], spread_recv.at[c, d], target
        )

    def spread_own(c):
        swap_copy(c).wait_recv()
        add(full, kept(c) + line * piece, landed_swap + c * piece, piece)

        @pl.when(has_above)
        def _():
            spread_copy(c, line, 0).start()

        @pl.when(has_below)
        def _():
            spread_copy(c, line, 1).start()

    def spread_rest(c):
        for k in range(1, length):
            for way, d, found in ((0, line - k, line >= k), (1, line + k, line + k < length)):
                @pl.when(found)
                def _(way=way, d=d):
                    spread_copy(c, d, way).wait_recv()

                    @pl.when(has_above if way == 0 else has_below)
                    def _():
                        spread_copy(c, d, way).start()

    def grow_copy(c):
        rows = pl.ds(pl.multiple_of(kept(c), 16), half)
        return remote(full.at[rows], full.at[rows], grow_send.at[c], grow_recv.at[c], partner)

    early = 3 * kv_heads // 8
    for c in chunks:
        core_copy(c).start()
    start_far(side == 0, range(early))

    @pl.when(crossing)
    def _():
        for head in range(direct, kv_heads):
            stage_copy(head).start()

    @pl.when(odd == 0)
    def _():
        for head in range(kv_heads):
            near_copy(head).start()

    for c in chunks:
        with jax.named_scope(f"core#c={c}"):
            core_copy(c).wait_recv()
            add(acc, kept(c), landed_core + c * half, half)
        with jax.named_scope(f"fold#c={c}"):
            fold_line(c)

    def queries(block, carry):
        rows = pl.ds(pl.multiple_of(block * BLOCK, BLOCK), BLOCK)
        for h in range(kv_heads * group_size):
            qs_ref[rows, h * head_dim : (h + 1) * head_dim] = q_ref[rows, h, :]
        return carry

    start_far(crossing, range(min(2, direct)))
    for c in chunks:
        with jax.named_scope(f"finish#c={c}"):
            finish_line(c)
        swap_copy(c).start()
    start_far(side == 0, range(early, kv_heads))
    with jax.named_scope("queries#p=0"):
        lax.fori_loop(0, per_dev // 2, queries, 0)
    for c in chunks:
        with jax.named_scope(f"swap#c={c}"):
            spread_own(c)
    with jax.named_scope("queries#p=1"):
        lax.fori_loop(per_dev // 2, per_dev, queries, 0)
    for c in chunks:
        with jax.named_scope(f"spread#c={c}"):
            spread_rest(c)
        grow_copy(c).start()
    start_far(crossing, range(min(2, direct), direct))
    pass_on(range(direct, kv_heads))

    heads_chunk = kv_heads // CHUNKS
    for head in range(kv_heads):
        with jax.named_scope(f"far#h={head}"):
            @pl.when(gets_far)
            def _():
                far_copy(head).wait_recv()

                @pl.when(odd == 1)
                def _():
                    relay_copy(head).start()

        with jax.named_scope(f"near#h={head}"):
            @pl.when((odd == 1) | gets_far)
            def _():
                near_copy(head).wait_recv()

        if head % heads_chunk == 0:
            with jax.named_scope(f"grow#h={head}"):
                grow_copy(head // heads_chunk).wait_recv()
        with jax.named_scope(f"attend#h={head}"):
            attend_head(
                head, dims, device, tables, qs_ref, windows[head], full, diagonal, unit, out_ref
            )

    @pl.when(sends_far)
    def _():
        for head in range(kv_heads):
            far_copy(head).wait_send()

    @pl.when((odd == 0) | gets_far)
    def _():
        for head in range(kv_heads):
            near_copy(head).wait_send()

    @pl.when(passes)
    def _():
        for head in range(direct, kv_heads):
            pass_copy(head).wait_send()

    for c in chunks:
        core_copy(c).wait_send()
        swap_copy(c).wait_send()
        grow_copy(c).wait_send()
        for d in range(length):
            @pl.when(line != d)
            def _(d=d):
                line_copy(c, d, 0).wait_send()

            @pl.when((line >= d) & has_above)
            def _(d=d):
                spread_copy(c, d, 0).wait_send()

            @pl.when((line <= d) & has_below)
            def _(d=d):
                spread_copy(c, d, 1).wait_send()


def fused(keys, values, queries, vert_blocks, vert_count, slash_offsets, slash_count):
    size = lax.axis_size("ctx")
    rows_dev, kv_heads, head_dim = keys.shape
    q_heads = queries.shape[1]
    per_dev = rows_dev // BLOCK
    n_vert = vert_blocks.shape[0]
    n_slash = slash_offsets.shape[0]
    reach = -(-LARGEST_OFFSET // per_dev)
    relayed = 3 * kv_heads // 8
    length = size // 4
    dims = (per_dev, reach, n_vert, n_slash, q_heads // kv_heads, head_dim)
    dma = pltpu.SemaphoreType.DMA
    kind = keys.dtype
    column_rows = kv_heads * n_vert * 2 * BLOCK
    columns = pltpu.VMEM((column_rows, head_dim), kind)
    landed_rows = column_rows + column_rows // 2 + column_rows // 2 // length
    square = pltpu.VMEM((BLOCK, BLOCK), kind)
    window = pltpu.VMEM(((reach + 1) * per_dev, 2, BLOCK, head_dim), kind)
    smem = pl.BlockSpec(memory_space=pltpu.SMEM)
    vmem = pl.BlockSpec(memory_space=pltpu.VMEM)
    return pl.pallas_call(
        functools.partial(fused_kernel, size, kv_heads, relayed, dims),
        out_shape=jax.ShapeDtypeStruct((rows_dev, q_heads * head_dim), kind),
        in_specs=[smem] * 4 + [vmem] * 3,
        out_specs=vmem,
        scratch_shapes=[
            pltpu.VMEM((kv_heads, per_dev, 2, BLOCK, head_dim), kind),
            pltpu.VMEM((rows_dev, q_heads * head_dim), kind),
            columns,
            pltpu.VMEM((landed_rows, head_dim), kind),
            columns,
            pltpu.VMEM((relayed, per_dev, 2, BLOCK, head_dim), kind),
            square,
            square,
        ]
        + [window] * kv_heads
        + [dma((CHUNKS,))] * 6
        + [dma((CHUNKS, length))] * 6
        + [dma((kv_heads,))] * 4
        + [dma((relayed,))] * 2,
        compiler_params=pltpu.CompilerParams(
            collective_id=0, has_side_effects=True, vmem_limit_bytes=40 * 1024 * 1024
        ),
        name="fused",
    )(vert_blocks, vert_count, slash_offsets, slash_count, keys, values, queries)


def local(
    query_states, key_states, value_states, vert_blocks, vert_count, slash_offsets, slash_count
):
    out = fused(
        key_states,
        value_states,
        query_states,
        vert_blocks.T,
        vert_count,
        slash_offsets.T,
        slash_count,
    )
    return out.reshape(query_states.shape)


def solution(mesh):
    in_specs = (
        P(("groups", "ctx"), None, None),
        P(("groups", "ctx"), None, None),
        P(("groups", "ctx"), None, None),
        P("groups", None),
        P("groups"),
        P("groups", None),
        P("groups"),
    )
    out_specs = P(("groups", "ctx"), None, None)
    return jax.shard_map(local, mesh=mesh, in_specs=in_specs, out_specs=out_specs, check_vma=False)
```

time: 129 us -> 98.4 us (0.76)
  Pallas kernels: 110 us -> 87 us
  local copies, waits for them, and re-layouts: 17.3 us -> 10.6 us
  other arithmetic: 1.51 us -> 0 us
    pallas_call x1, Pallas kernels: 110 us -> 87 us  [fused(): pl.pallas_call(functools.partial(fused_kernel, size, kv_heads, relayed, d...]
    unnamed x8 -> x15, local copies, waits for them, and re-layouts: 17.3 us -> 10.6 us
    another operation x1 -> x0, other arithmetic: 1.51 us -> none  [local(): own = jnp.stack((by_tile(key_states), by_tile(value_states)), axis=2)]
where the time goes in v2:
time: 98.4 us; the launch traced here: 97.6 us
  Pallas kernels  87 us (88%)
  local copies, waits for them, and re-layouts  10.6 us (11%)
    pallas_call x1, Pallas kernels, fused(): pl.pallas_call(functools.partial(fused_kernel, size, kv_heads, relayed, d...  87 us
    unnamed x15, local copies, waits for them, and re-layouts  10.6 us

profile of v2, /device:TPU:24, one launch (start us, length us, event | category | flops | bytes accessed | tf_op | source)
XLA Modules:
  0.0 97.6 jit_solution(7014299531061722285)
XLA Ops:
  0.0 0.0 copy-start
  0.0 2.2 %copy-done = bf16[512,32,128]{2,1,0:T(8,128)(2,1)S(1)} copy-done((bf16[512,32,128]{2,1,0:T(8,128)(2,1)S(1)}, bf16[512,32,128]{2,1,0:T(8,128)(2,1)}, u32[]{:S(2)}) %copy-start) | copy-done | bytes 4194328
  2.2 0.0 copy-start.1
  2.2 1.2 %copy-done.1 = bf16[512,8,128]{2,1,0:T(8,128)(2,1)S(1)} copy-done((bf16[512,8,128]{2,1,0:T(8,128)(2,1)S(1)}, bf16[512,8,128]{2,1,0:T(8,128)(2,1)}, u32[]{:S(2)}) %copy-start.1) | copy-done | bytes 1048600
  3.4 0.0 copy-start.2
  3.4 1.2 %copy-done.2 = bf16[512,8,128]{2,1,0:T(8,128)(2,1)S(1)} copy-done((bf16[512,8,128]{2,1,0:T(8,128)(2,1)S(1)}, bf16[512,8,128]{2,1,0:T(8,128)(2,1)}, u32[]{:S(2)}) %copy-start.2) | copy-done | bytes 1048600
  4.6 0.0 copy-start.3
  4.6 0.7 copy-done.3
  5.3 0.0 copy-start.4
  5.3 0.7 copy-done.4
  6.0 0.0 copy-start.5
  6.0 0.7 copy-done.5
  6.7 0.0 copy-start.6
  6.7 0.7 copy-done.6
  7.3 87.0 %fused.1 = bf16[512,4096]{1,0:T(8,128)(2,1)S(1)} custom-call(s32[4,8]{1,0:T(4,128)S(1)} %bitcast.5, s32[8]{0:T(128)S(1)} %copy-done.5, s32[4,8]{1,0:T(4,128)S(1)} %bitcast.6, s32[8]{0:T(128)S(1)} %copy-done.6, bf16[512,8,128]{2,1,0:T(8,128)(2,1)S(1)} %copy-done.1, bf16[512,8,128]{2,1,0:T(8,128)(2,1)S(1)} %copy-done.2, bf16[512,32,128]{2,1,0:T(8,128)(2,1)S(1)} %copy-done), custom_call_target="tpu_custom_call" | custom-call | tf_op jit(solution)/shard_map/fused/pallas_call | solution.py:475
  94.3 3.3 %copy.8 = bf16[64,8,32,128]{3,2,1,0:T(8,128)(2,1)} copy(bf16[64,8,32,128]{3,1,2,0:T(8,128)(2,1)S(1)} %bitcast.4) | data formatting | bytes 8388608
Async XLA Ops:
  0.0 2.2 %copy-start = (bf16[512,32,128]{2,1,0:T(8,128)(2,1)S(1)}, bf16[512,32,128]{2,1,0:T(8,128)(2,1)}, u32[]{:S(2)}) copy-start(bf16[512,32,128]{2,1,0:T(8,128)(2,1)} %q_ref.1) | copy-start | bytes 12582916
  2.2 1.2 %copy-start.1 = (bf16[512,8,128]{2,1,0:T(8,128)(2,1)S(1)}, bf16[512,8,128]{2,1,0:T(8,128)(2,1)}, u32[]{:S(2)}) copy-start(bf16[512,8,128]{2,1,0:T(8,128)(2,1)} %k_ref.1) | copy-start | bytes 3145732
  3.4 1.2 %copy-start.2 = (bf16[512,8,128]{2,1,0:T(8,128)(2,1)S(1)}, bf16[512,8,128]{2,1,0:T(8,128)(2,1)}, u32[]{:S(2)}) copy-start(bf16[512,8,128]{2,1,0:T(8,128)(2,1)} %v_ref.1) | copy-start | bytes 3145732
  4.6 0.7 copy-start.3
  5.3 0.7 copy-start.4
  6.0 0.7 copy-start.5
  6.7 0.7 copy-start.6

commit v3 on v2

--- a/solution.py
+++ b/solution.py
@@ -99,13 +99,13 @@
 
 def fused_kernel(
     size, kv_heads, relayed, dims,
-    vb_ref, vc_ref, so_ref, sc_ref, k_ref, v_ref, q_ref, out_ref,
-    own_ref, qs_ref, acc, landed, full, stage, diagonal, unit, *scratch,
+    vb_hbm, vc_hbm, so_hbm, sc_hbm, k_hbm, v_hbm, q_hbm, out_hbm,
+    vb_ref, vc_ref, so_ref, sc_ref, k_ref, v_ref, q_ref, out_ref, own_ref, qs_ref, acc, landed, full, stage, diagonal, unit, *scratch,
 ):
     per_dev, reach, n_vert, n_slash, group_size, head_dim = dims
     windows = scratch[:kv_heads]
     (
-        core_send, core_recv, grow_send, grow_recv, swap_send, swap_recv,
+        load_sem, out_sem, core_send, core_recv, grow_send, grow_recv, swap_send, swap_recv,
         up_recv, down_recv, line_send, spread_recv, above_send, below_send,
         far_send, far_recv, near_send, near_recv, pass_send, pass_recv,
     ) = scratch[kv_heads:]
@@ -124,6 +124,16 @@
             device_id={"ctx": target}, device_id_type=pl.DeviceIdType.MESH,
         )
 
+    loads = [
+        pltpu.make_async_copy(src, dst, load_sem.at[i])
+        for i, (src, dst) in enumerate((
+            (k_hbm, k_ref), (v_hbm, v_ref), (vb_hbm, vb_ref), (vc_hbm, vc_ref),
+            (so_hbm, so_ref), (sc_hbm, sc_ref), (q_hbm, q_ref),
+        ))
+    ]
+    for load in loads:
+        load.start()
+
     sends_far = device + reach < size
     gets_far = device >= reach
     crossing = (side == 1) & sends_far
@@ -171,6 +181,9 @@
                 windows[head][reach * per_dev + block, kv] = tile
         return carry
 
+    with jax.named_scope("loads"):
+        for load in loads[:-1]:
+            load.wait()
     with jax.named_scope("own"):
         lax.fori_loop(0, per_dev, own_block, 0)
 
@@ -224,8 +237,8 @@
             for head in heads:
                 far_copy(head).start()
 
-    def pass_on(heads):
-        @pl.when(passes)
+    def pass_on(condition, heads):
+        @pl.when(passes & condition)
         def _():
             for head in heads:
                 with jax.named_scope(f"stage#h={head}"):
@@ -279,7 +292,7 @@
         line_copy(c, d, way).wait_recv()
         add(acc, kept(c) + d * piece, ((c * length + d) * 2 + way) * piece, piece)
 
-    def fold_line(c):
+    def fold_up(c):
         for d in range(length - 1, 0, -1):
             @pl.when(line < d)
             def _(d=d):
@@ -289,6 +302,7 @@
 
                 line_copy(c, d, 0).start()
 
+    def fold_down(c):
         for d in range(length - 1):
             @pl.when(line > d)
             def _(d=d):
@@ -298,6 +312,19 @@
 
                 line_copy(c, d, 1).start()
 
+    lower = 2 * line < length
+
+    def fold_line(c):
+        @pl.when(lower)
+        def _():
+            fold_up(c)
+            fold_down(c)
+
+        @pl.when(jnp.logical_not(lower))
+        def _():
+            fold_down(c)
+            fold_up(c)
+
     def finish_line(c):
         @pl.when(has_below)
         def _():
@@ -347,15 +374,21 @@
         rows = pl.ds(pl.multiple_of(kept(c), 16), half)
         return remote(full.at[rows], full.at[rows], grow_send.at[c], grow_recv.at[c], partner)
 
-    early = 3 * kv_heads // 8
+    early = kv_heads // 4
+    middle = has_above & has_below
+    edge = jnp.logical_not(middle)
+
+    def stage_on(heads):
+        @pl.when(crossing)
+        def _():
+            for head in heads:
+                stage_copy(head).start()
+
     for c in chunks:
         core_copy(c).start()
     start_far(side == 0, range(early))
-
-    @pl.when(crossing)
-    def _():
-        for head in range(direct, kv_heads):
-            stage_copy(head).start()
+    stage_on(range(direct, direct + 2))
+    start_far(crossing & (line == length - 2) & (line > 0), range(2))
 
     @pl.when(odd == 0)
     def _():
@@ -366,8 +399,9 @@
         with jax.named_scope(f"core#c={c}"):
             core_copy(c).wait_recv()
             add(acc, kept(c), landed_core + c * half, half)
-        with jax.named_scope(f"fold#c={c}"):
-            fold_line(c)
+        if c == 0:
+            with jax.named_scope(f"fold#c={c}"):
+                fold_line(c)
 
     def queries(block, carry):
         rows = pl.ds(pl.multiple_of(block * BLOCK, BLOCK), BLOCK)
@@ -375,28 +409,48 @@
             qs_ref[rows, h * head_dim : (h + 1) * head_dim] = q_ref[rows, h, :]
         return carry
 
-    start_far(crossing, range(min(2, direct)))
-    for c in chunks:
-        with jax.named_scope(f"finish#c={c}"):
-            finish_line(c)
-        swap_copy(c).start()
-    start_far(side == 0, range(early, kv_heads))
+    @pl.when(edge)
+    def _():
+        with jax.named_scope("fold_edge#c=1"):
+            fold_line(1)
+
+    with jax.named_scope("finish#c=0"):
+        finish_line(0)
+    swap_copy(0).start()
+    stage_on(range(direct + 2, direct + 3))
+    pass_on((line == length - 2) & (line > 0), range(direct, direct + 2))
+
+    @pl.when(middle)
+    def _():
+        with jax.named_scope("fold_mid#c=1"):
+            fold_line(1)
+
+    loads[-1].wait()
     with jax.named_scope("queries#p=0"):
         lax.fori_loop(0, per_dev // 2, queries, 0)
-    for c in chunks:
-        with jax.named_scope(f"swap#c={c}"):
-            spread_own(c)
+    with jax.named_scope("swap#c=0"):
+        spread_own(0)
+    with jax.named_scope("finish#c=1"):
+        finish_line(1)
+    swap_copy(1).start()
+    start_far(side == 0, range(early, kv_heads))
+    stage_on(range(direct + 3, kv_heads))
     with jax.named_scope("queries#p=1"):
         lax.fori_loop(per_dev // 2, per_dev, queries, 0)
-    for c in chunks:
-        with jax.named_scope(f"spread#c={c}"):
-            spread_rest(c)
-        grow_copy(c).start()
-    start_far(crossing, range(min(2, direct), direct))
-    pass_on(range(direct, kv_heads))
+    with jax.named_scope("swap#c=1"):
+        spread_own(1)
+    late = (line != length - 2) | (line == 0)
+    start_far(crossing & (line == 0), range(2))
+    pass_on(line == 0, range(direct, direct + 2))
+    with jax.named_scope("spread#c=0"):
+        spread_rest(0)
+    grow_copy(0).start()
+    start_far(crossing & late & (line > 0), range(1))
+    pass_on(late & (line > 0), range(direct, direct + 1))
 
     heads_chunk = kv_heads // CHUNKS
-    for head in range(kv_heads):
+
+    def get_head(head):
         with jax.named_scope(f"far#h={head}"):
             @pl.when(gets_far)
             def _():
@@ -411,13 +465,39 @@
             def _():
                 near_copy(head).wait_recv()
 
-        if head % heads_chunk == 0:
-            with jax.named_scope(f"grow#h={head}"):
-                grow_copy(head // heads_chunk).wait_recv()
+    def out_copy(head):
+        lanes = pl.ds(head * group_size * head_dim, group_size * head_dim)
+        return pltpu.make_async_copy(out_ref.at[:, lanes], out_hbm.at[:, lanes], out_sem.at[head])
+
+    def do_head(head):
         with jax.named_scope(f"attend#h={head}"):
             attend_head(
                 head, dims, device, tables, qs_ref, windows[head], full, diagonal, unit, out_ref
             )
+        out_copy(head).start()
+
+    with jax.named_scope("spread#c=1"):
+        spread_rest(1)
+    grow_copy(1).start()
+    start_far(crossing & late & (line > 0), range(1, 2))
+    pass_on(late & (line > 0), range(direct + 1, direct + 2))
+    start_far(crossing, range(2, direct))
+    with jax.named_scope("grow#c=0"):
+        grow_copy(0).wait_recv()
+
+    order = [h for i in range(kv_heads) for h in (i, direct + i) if i < direct and h < kv_heads]
+    for head in order:
+        get_head(head)
+        if head == next(h for h in order if h >= heads_chunk):
+            with jax.named_scope("grow#c=1"):
+                grow_copy(1).wait_recv()
+        do_head(head)
+        step = order.index(head)
+        if step >= 1 and direct + 1 + step < kv_heads:
+            pass_on(line >= 0, range(direct + 1 + step, direct + 2 + step))
+
+    for head in range(kv_heads):
+        out_copy(head).wait()
 
     @pl.when(sends_far)
     def _():
@@ -460,7 +540,7 @@
     n_vert = vert_blocks.shape[0]
     n_slash = slash_offsets.shape[0]
     reach = -(-LARGEST_OFFSET // per_dev)
-    relayed = 3 * kv_heads // 8
+    relayed = kv_heads // 2
     length = size // 4
     dims = (per_dev, reach, n_vert, n_slash, q_heads // kv_heads, head_dim)
     dma = pltpu.SemaphoreType.DMA
@@ -470,14 +550,21 @@
     landed_rows = column_rows + column_rows // 2 + column_rows // 2 // length
     square = pltpu.VMEM((BLOCK, BLOCK), kind)
     window = pltpu.VMEM(((reach + 1) * per_dev, 2, BLOCK, head_dim), kind)
-    smem = pl.BlockSpec(memory_space=pltpu.SMEM)
-    vmem = pl.BlockSpec(memory_space=pltpu.VMEM)
+    hbm = pl.BlockSpec(memory_space=pltpu.HBM)
     return pl.pallas_call(
         functools.partial(fused_kernel, size, kv_heads, relayed, dims),
         out_shape=jax.ShapeDtypeStruct((rows_dev, q_heads * head_dim), kind),
-        in_specs=[smem] * 4 + [vmem] * 3,
-        out_specs=vmem,
+        in_specs=[hbm] * 7,
+        out_specs=hbm,
         scratch_shapes=[
+            pltpu.SMEM(vert_blocks.shape, jnp.int32),
+            pltpu.SMEM(vert_count.shape, jnp.int32),
+            pltpu.SMEM(slash_offsets.shape, jnp.int32),
+            pltpu.SMEM(slash_count.shape, jnp.int32),
+            pltpu.VMEM(keys.shape, kind),
+            pltpu.VMEM(values.shape, kind),
+            pltpu.VMEM(queries.shape, kind),
+            pltpu.VMEM((rows_dev, q_heads * head_dim), kind),
             pltpu.VMEM((kv_heads, per_dev, 2, BLOCK, head_dim), kind),
             pltpu.VMEM((rows_dev, q_heads * head_dim), kind),
             columns,
@@ -488,12 +575,13 @@
             square,
         ]
         + [window] * kv_heads
+        + [dma((7,)), dma((kv_heads,))]
         + [dma((CHUNKS,))] * 6
         + [dma((CHUNKS, length))] * 6
         + [dma((kv_heads,))] * 4
         + [dma((relayed,))] * 2,
         compiler_params=pltpu.CompilerParams(
-            collective_id=0, has_side_effects=True, vmem_limit_bytes=40 * 1024 * 1024
+            collective_id=0, has_side_effects=True, vmem_limit_bytes=56 * 1024 * 1024
         ),
         name="fused",
     )(vert_blocks, vert_count, slash_offsets, slash_count, keys, values, queries)

time: 98.4 us -> 88 us (0.89)
  local copies, waits for them, and re-layouts: 10.6 us -> 5.48 us
  Pallas kernels: 87 us -> 82 us
    unnamed x15 -> x1, local copies, waits for them, and re-layouts: 10.6 us -> 5.48 us
    pallas_call x1, Pallas kernels: 87 us -> 82 us  [fused(): pl.pallas_call(functools.partial(fused_kernel, size, kv_heads, relayed, d...]
where the time goes in v3:
time: 88 us; the launch traced here: 87.5 us
  Pallas kernels  82 us (93%)
  local copies, waits for them, and re-layouts  5.48 us (6%)
    pallas_call x1, Pallas kernels, fused(): pl.pallas_call(functools.partial(fused_kernel, size, kv_heads, relayed, d...  82 us
    unnamed x1, local copies, waits for them, and re-layouts  5.48 us

profile of v3, /device:TPU:24, one launch (start us, length us, event | category | flops | bytes accessed | tf_op | source)
XLA Modules:
  0.0 87.5 jit_solution(11549570633911995784)
XLA Ops:
  0.0 82.0 %fused.1 = bf16[512,4096]{1,0:T(8,128)(2,1)} custom-call(s32[4,8]{1,0:T(4,128)} %bitcast.5, s32[8]{0:T(128)} %vc_hbm.1, s32[4,8]{1,0:T(4,128)} %bitcast.6, s32[8]{0:T(128)} %sc_hbm.1, bf16[512,8,128]{2,1,0:T(8,128)(2,1)} %k_hbm.1, bf16[512,8,128]{2,1,0:T(8,128)(2,1)} %v_hbm.1, bf16[512,32,128]{2,1,0:T(8,128)(2,1)} %q_hbm.1), custom_call_target="tpu_custom_call" | custom-call | tf_op jit(solution)/shard_map/fused/pallas_call | solution.py:554
  82.0 5.5 %copy.8 = bf16[64,8,32,128]{3,2,1,0:T(8,128)(2,1)} copy(bf16[64,8,32,128]{3,1,2,0:T(8,128)(2,1)} %bitcast.4) | data formatting | bytes 8388608

commit v4 on v3

--- a/solution.py
+++ b/solution.py
@@ -414,6 +414,13 @@
         with jax.named_scope("fold_edge#c=1"):
             fold_line(1)
 
+    loads[-1].wait()
+
+    @pl.when(edge)
+    def _():
+        with jax.named_scope("queries_edge"):
+            lax.fori_loop(0, per_dev, queries, 0)
+
     with jax.named_scope("finish#c=0"):
         finish_line(0)
     swap_copy(0).start()
@@ -425,9 +432,6 @@
         with jax.named_scope("fold_mid#c=1"):
             fold_line(1)
 
-    loads[-1].wait()
-    with jax.named_scope("queries#p=0"):
-        lax.fori_loop(0, per_dev // 2, queries, 0)
     with jax.named_scope("swap#c=0"):
         spread_own(0)
     with jax.named_scope("finish#c=1"):
@@ -435,8 +439,12 @@
     swap_copy(1).start()
     start_far(side == 0, range(early, kv_heads))
     stage_on(range(direct + 3, kv_heads))
-    with jax.named_scope("queries#p=1"):
-        lax.fori_loop(per_dev // 2, per_dev, queries, 0)
+
+    @pl.when(middle)
+    def _():
+        with jax.named_scope("queries#p=0"):
+            lax.fori_loop(0, per_dev // 2, queries, 0)
+
     with jax.named_scope("swap#c=1"):
         spread_own(1)
     late = (line != length - 2) | (line == 0)
@@ -448,6 +456,12 @@
     start_far(crossing & late & (line > 0), range(1))
     pass_on(late & (line > 0), range(direct, direct + 1))
 
+    @pl.when(middle)
+    def _():
+        with jax.named_scope("queries#p=1"):
+            lax.fori_loop(per_dev // 2, per_dev, queries, 0)
+
+
     heads_chunk = kv_heads // CHUNKS
 
     def get_head(head):
@@ -476,25 +490,43 @@
             )
         out_copy(head).start()
 
+    def do_first(heads):
+        with jax.named_scope("grow#c=0"):
+            grow_copy(0).wait_recv()
+        for head in heads:
+            get_head(head)
+            do_head(head)
+
+    @pl.when(edge)
+    def _():
+        do_first(range(2))
+
     with jax.named_scope("spread#c=1"):
         spread_rest(1)
     grow_copy(1).start()
     start_far(crossing & late & (line > 0), range(1, 2))
     pass_on(late & (line > 0), range(direct + 1, direct + 2))
     start_far(crossing, range(2, direct))
-    with jax.named_scope("grow#c=0"):
-        grow_copy(0).wait_recv()
-
+
+    @pl.when(middle)
+    def _():
+        do_first(range(1))
+
+    with jax.named_scope("grow#c=1"):
+        grow_copy(1).wait_recv()
     order = [h for i in range(kv_heads) for h in (i, direct + i) if i < direct and h < kv_heads]
-    for head in order:
+    order = [h for h in order if h > 1]
+    for step, head in enumerate(order):
         get_head(head)
-        if head == next(h for h in order if h >= heads_chunk):
-            with jax.named_scope("grow#c=1"):
-                grow_copy(1).wait_recv()
         do_head(head)
-        step = order.index(head)
-        if step >= 1 and direct + 1 + step < kv_heads:
-            pass_on(line >= 0, range(direct + 1 + step, direct + 2 + step))
+        if step == 0:
+            @pl.when(middle)
+            def _():
+                get_head(1)
+                do_head(1)
+
+        if direct + 2 + step < kv_heads:
+            pass_on(line >= 0, range(direct + 2 + step, direct + 3 + step))
 
     for head in range(kv_heads):
         out_copy(head).wait()

time: 88 us -> 85.9 us (0.976)
  Pallas kernels: 82 us -> 80.3 us
    pallas_call x1, Pallas kernels: 82 us -> 80.3 us  [fused(): pl.pallas_call(functools.partial(fused_kernel, size, kv_heads, relayed, d...]
where the time goes in v4:
time: 85.9 us; the launch traced here: 85.7 us
  Pallas kernels  80.3 us (93%)
  local copies, waits for them, and re-layouts  5.48 us (6%)
    pallas_call x1, Pallas kernels, fused(): pl.pallas_call(functools.partial(fused_kernel, size, kv_heads, relayed, d...  80.3 us
    unnamed x1, local copies, waits for them, and re-layouts  5.48 us

profile of v4, /device:TPU:24, one launch (start us, length us, event | category | flops | bytes accessed | tf_op | source)
XLA Modules:
  0.0 85.7 jit_solution(920873839113737444)
XLA Ops:
  0.0 80.3 %fused.1 = bf16[512,4096]{1,0:T(8,128)(2,1)} custom-call(s32[4,8]{1,0:T(4,128)} %bitcast.5, s32[8]{0:T(128)} %vc_hbm.1, s32[4,8]{1,0:T(4,128)} %bitcast.6, s32[8]{0:T(128)} %sc_hbm.1, bf16[512,8,128]{2,1,0:T(8,128)(2,1)} %k_hbm.1, bf16[512,8,128]{2,1,0:T(8,128)(2,1)} %v_hbm.1, bf16[512,32,128]{2,1,0:T(8,128)(2,1)} %q_hbm.1), custom_call_target="tpu_custom_call" | custom-call | tf_op jit(solution)/shard_map/fused/pallas_call | solution.py:586
  80.3 5.5 %copy.8 = bf16[64,8,32,128]{3,2,1,0:T(8,128)(2,1)} copy(bf16[64,8,32,128]{3,1,2,0:T(8,128)(2,1)} %bitcast.4) | data formatting | bytes 8388608

commit v5 on v4

--- a/solution.py
+++ b/solution.py
@@ -450,6 +450,13 @@
     late = (line != length - 2) | (line == 0)
     start_far(crossing & (line == 0), range(2))
     pass_on(line == 0, range(direct, direct + 2))
+
+    @pl.when(edge & gets_far & (odd == 1))
+    def _():
+        for head in range(2):
+            far_copy(head).wait_recv()
+            relay_copy(head).start()
+
     with jax.named_scope("spread#c=0"):
         spread_rest(0)
     grow_copy(0).start()
@@ -464,15 +471,16 @@
 
     heads_chunk = kv_heads // CHUNKS
 
-    def get_head(head):
+    def get_head(head, handed=False):
         with jax.named_scope(f"far#h={head}"):
-            @pl.when(gets_far)
+            @pl.when(gets_far & (odd == 0) if handed else gets_far)
             def _():
                 far_copy(head).wait_recv()
 
-                @pl.when(odd == 1)
-                def _():
-                    relay_copy(head).start()
+                if not handed:
+                    @pl.when(odd == 1)
+                    def _():
+                        relay_copy(head).start()
 
         with jax.named_scope(f"near#h={head}"):
             @pl.when((odd == 1) | gets_far)
@@ -490,16 +498,16 @@
             )
         out_copy(head).start()
 
-    def do_first(heads):
+    def do_first(heads, handed):
         with jax.named_scope("grow#c=0"):
             grow_copy(0).wait_recv()
         for head in heads:
-            get_head(head)
+            get_head(head, handed)
             do_head(head)
 
     @pl.when(edge)
     def _():
-        do_first(range(2))
+        do_first(range(2), True)
 
     with jax.named_scope("spread#c=1"):
         spread_rest(1)
@@ -510,7 +518,7 @@
 
     @pl.when(middle)
     def _():
-        do_first(range(1))
+        do_first(range(1), False)
 
     with jax.named_scope("grow#c=1"):
         grow_copy(1).wait_recv()

time: 85.9 us -> 85.9 us (level)
  no operation moved by 1% of the time
where the time goes in v5:
time: 85.9 us; the launch traced here: 85.7 us
  Pallas kernels  80.3 us (93%)
  local copies, waits for them, and re-layouts  5.48 us (6%)
    pallas_call x1, Pallas kernels, fused(): pl.pallas_call(functools.partial(fused_kernel, size, kv_heads, relayed, d...  80.3 us
    unnamed x1, local copies, waits for them, and re-layouts  5.48 us

profile of v5, /device:TPU:24, one launch (start us, length us, event | category | flops | bytes accessed | tf_op | source)
XLA Modules:
  0.0 85.7 jit_solution(14408645040010675627)
XLA Ops:
  0.0 80.3 %fused.1 = bf16[512,4096]{1,0:T(8,128)(2,1)} custom-call(s32[4,8]{1,0:T(4,128)} %bitcast.5, s32[8]{0:T(128)} %vc_hbm.1, s32[4,8]{1,0:T(4,128)} %bitcast.6, s32[8]{0:T(128)} %sc_hbm.1, bf16[512,8,128]{2,1,0:T(8,128)(2,1)} %k_hbm.1, bf16[512,8,128]{2,1,0:T(8,128)(2,1)} %v_hbm.1, bf16[512,32,128]{2,1,0:T(8,128)(2,1)} %q_hbm.1), custom_call_target="tpu_custom_call" | custom-call | tf_op jit(solution)/shard_map/fused/pallas_call | solution.py:594
  80.3 5.5 %copy.8 = bf16[64,8,32,128]{3,2,1,0:T(8,128)(2,1)} copy(bf16[64,8,32,128]{3,1,2,0:T(8,128)(2,1)} %bitcast.4) | data formatting | bytes 8388608
